TPU v7x, 256 devices: a whole 4x4x8 slice. The times are simulated.
256 devices in a mesh: sub: 64 (over z, y, core), grp: 4 (over x).
Axes of the slice: x: 4, y: 4, z: 8, core: 2. Of those that a mesh axis runs over, the one named last changes fastest.
Arguments:
- interior_factor: bfloat16 [256, 2048, 2048], P(('sub', 'grp')), may hold values from -0.25 to 2, as said below
- interface_coupling: bfloat16 [256, 2048, 512], P(('sub', 'grp')), may hold values from -0.09375 to 0.09375
- interface_block: float32 [256, 512, 512], P(('sub', 'grp')), may hold values from -0.5 to 4, as said below
- sample_panel: bfloat16 [32768, 128], P('sub'), may hold values from -6 to 6
- index_map: int32 [256, 4], P(('sub', 'grp')), may hold values from 0 to 255, as said below
- block_count: int32 [256], P(('sub', 'grp')), may hold values from 1 to 4
Outputs:
- sampled: float32 [32768, 128], P(('sub', 'grp'))
Inputs may be any that keep to these rules, and one draw needn't show every extreme that they name: `index_map`: local block a of subdomain s is global block o * 4 + a, where o is s // 4, or one more or one less than it modulo 256 // 4. `interior_factor`: each matrix is lower triangular with its diagonal in 1 to 2. `interface_block`: each matrix is symmetric with its diagonal in 2 to 4.
All inputs are finite; a program needn't handle non-finite values.
Results may differ from a plain program's by a relative error of at most 0.0012.
Values sent between devices are 32-bit elements; how exact they have to be, the bound alone decides.
A program may use at most 64 MiB of HBM per device.

v0:
```python
import jax
import jax.numpy as jnp
from jax import lax
from jax.sharding import PartitionSpec as P

POWER = 3


def joined_along(tiles, dim):
    lengths = list(tiles.shape[1:])
    lengths[dim] *= tiles.shape[0]
    return jnp.moveaxis(tiles, 0, dim).reshape(lengths)


def sent_to_all(value, axis):
    copies = jnp.broadcast_to(value, (lax.axis_size(axis), *value.shape))
    return lax.all_to_all(copies, axis, split_axis=0, concat_axis=0, tiled=True)


def gather_directly(value, axis, dim):
    return joined_along(sent_to_all(value, axis), dim)


def passed_along(block, axis, distance):
    devices = range(lax.axis_size(axis))
    route = [((i - distance) % len(devices), i) for i in devices]
    return lax.ppermute(block, axis, route)


def spread_rows(block):
    return gather_directly(block, "grp", 0)


def local(
    interior_factor, interface_coupling, interface_block, sample_panel, index_map, block_count
):
    factor = interior_factor[0]
    coupling = interface_coupling[0]
    coupled = jnp.dot(factor, coupling, preferred_element_type=jnp.float32).astype(jnp.bfloat16)
    gram = lax.dot_general(
        coupled, coupled, (((0,), (0,)), ((), ())), preferred_element_type=jnp.float32
    )
    schur = interface_block[0] - gram
    ids = index_map[0]
    count = block_count[0]
    nblk = ids.shape[0]
    width = schur.shape[0]
    blk = width // nblk
    samples = sample_panel.shape[1]
    cycles = lax.axis_size("sub")
    groups = lax.axis_size("grp")
    home = lax.axis_index("sub")
    live = (jnp.arange(nblk, dtype=jnp.int32) < count).astype(jnp.float32)
    masked = (
        schur.reshape(nblk, blk, nblk, blk) * live[:, None, None, None] * live[None, None, :, None]
    )
    owners = ids // groups
    dest = (owners - home + cycles + 1) % cycles - 1
    current = sample_panel.astype(jnp.float32)
    column = (dest + 1) * groups + ids % groups
    frame = jnp.arange(3 * groups, dtype=jnp.int32)
    selector = (column[:, None] == frame[None, :]).astype(jnp.float32)
    flat = masked.reshape(width, width)
    result = None
    for step in range(POWER):
        pieces = []
        for offset in (-1, 0, 1):
            if offset == 0:
                pieces.append(current)
            else:
                pieces.append(passed_along(current, "sub", -offset))
        near = jnp.concatenate(pieces, axis=0).reshape(3 * groups, blk, samples)
        picked = jnp.einsum("bq,qcn->bcn", selector, near, precision=lax.Precision.HIGHEST)
        product = jnp.dot(flat, picked.reshape(width, samples), precision=lax.Precision.HIGHEST)
        product = product.reshape(nblk, blk, samples)
        got_terms, got_dest = (
            lax.all_to_all(product, "grp", split_axis=0, concat_axis=0, tiled=True),
            lax.all_to_all(
                dest.astype(jnp.float32), "grp", split_axis=0, concat_axis=0, tiled=True
            ),
        )
        total = jnp.sum(got_terms * (got_dest == 0).astype(jnp.float32)[:, None, None], axis=0)
        for offset in (-1, 1):
            keep = (got_dest == offset).astype(jnp.float32)[:, None, None]
            summed = jnp.sum(got_terms * keep, axis=0)
            total = total + passed_along(summed, "sub", offset)
        result = 0.5 * total
        if step + 1 < POWER:
            current = spread_rows(result)
    return result


def solution(mesh):
    return jax.shard_map(
        local,
        mesh=mesh,
        in_specs=(
            P(("sub", "grp"), None, None),
            P(("sub", "grp"), None, None),
            P(("sub", "grp"), None, None),
            P("sub", None),
            P(("sub", "grp"), None),
            P(("sub", "grp")),
        ),
        out_specs=P(("sub", "grp"), None),
        check_vma=False,
    )
```

profile of v0, /device:TPU:2, one launch (start us, length us, event | category | flops | bytes accessed | tf_op | source)
XLA Modules:
  0.0 129.7 jit_solution(1589104447060363336)
XLA Ops:
  0.0 1.1 convert_element_type.44
  1.1 7.8 %collective-permute-start.1 = (f32[512,128]{1,0:T(8,128)S(1)}, f32[512,128]{1,0:T(8,128)}, u32[]{:S(2)}, u32[]{:S(2)}) collective-permute-start(f32[512,128]{1,0:T(8,128)S(1)} %convert_element_type.44), channel_id=1, source_target_pairs={{4,0},{8,4},{12,8},{16,12},{20,16},{24,20},{28,24},{32,28},{36,32}... | collective-permute-start | bytes 786440 | tf_op jit(solution)/shard_map/ppermute | solution.py:27
  10.2 4.8 %all-to-all-start.1 = ((f32[4,1,1]{2,1,0:T(1,128)}), f32[4,1,1]{2,1,0:T(1,128)S(1)}, u32[]{:S(2)}, u32[]{:S(2)}) async-start(f32[4,1,1]{2,1,0:T(1,128)} %copy.22), calls=%async_computation.1 | async-start | bytes 4096 | tf_op jit(solution)/shard_map/all_to_all | solution.py:78
  15.8 16.0 %fusion.7 = f32[512,512]{1,0:T(8,128)S(1)} fusion(bf16[1,2048,2048]{2,1,0:T(8,128)(2,1)} %param.6, bf16[1,2048,512]{2,1,0:T(8,128)(2,1)S(1)} %copy-done, f32[1,512,512]{2,1,0:T(8,128)} %param.8, f32[512]{0:T(512)S(1)} %broadcast_bitcast_fusion), kind=kOutput, calls=%fused_computation.6 | convolution fusion | flops 5370544128 | bytes 12584960 | tf_op jit(solution)/shard_map/dot_general | solution.py:40
  31.9 1.1 pad_maximum_fusion
  33.9 1.7 %fusion.31 = f32[4,128,128]{2,1,0:T(8,128)} fusion(f32[4,128,512]{2,1,0:T(8,128)S(1)} %bitcast.67, f32[512,128,1]{1,0,2:T(8,128)S(1)} %bitcast.80), kind=kOutput, calls=%fused_computation.61 | convolution fusion | flops 402653184 | bytes 1572864 | tf_op jit(solution)/shard_map/dot_general | solution.py:74
  35.6 4.8 %all-to-all-start = ((f32[4,128,128]{2,1,0:T(8,128)}), f32[4,128,128]{2,1,0:T(8,128)S(1)}, u32[]{:S(2)}, u32[]{:S(2)}) async-start(f32[4,128,128]{2,1,0:T(8,128)} %fusion.31), calls=%async_computation | async-start | bytes 524288 | tf_op jit(solution)/shard_map/all_to_all | solution.py:77
  40.5 5.1 %all-to-all-done = f32[4,128,128]{2,1,0:T(8,128)S(1)} async-done(((f32[4,128,128]{2,1,0:T(8,128)}), f32[4,128,128]{2,1,0:T(8,128)S(1)}, u32[]{:S(2)}, u32[]{:S(2)}) %all-to-all-start) | async-done | bytes 262176 | tf_op jit(solution)/shard_map/all_to_all | solution.py:77
  45.7 3.1 %collective-permute-start.2 = (f32[128,128]{1,0:T(8,128)S(1)}, f32[128,128]{1,0:T(8,128)S(1)}, u32[]{:S(2)}, u32[]{:S(2)}) collective-permute-start(f32[128,128]{1,0:T(8,128)S(1)} %get-tuple-element.11), channel_id=1, source_target_pairs={{4,0},{8,4},{12,8},{16,12},{20,16},{24,20},{28,24},{32,28},{36,32}... | collective-permute-start | bytes 196616 | tf_op jit(solution)/shard_map/ppermute | solution.py:27
  48.8 1.9 %collective-permute-done.2 = f32[128,128]{1,0:T(8,128)S(1)} collective-permute-done((f32[128,128]{1,0:T(8,128)S(1)}, f32[128,128]{1,0:T(8,128)S(1)}, u32[]{:S(2)}, u32[]{:S(2)}) %collective-permute-start.2) | collective-permute-done | bytes 65568 | tf_op jit(solution)/shard_map/ppermute | solution.py:27
  50.7 5.1 %collective-permute-done.3 = f32[128,128]{1,0:T(8,128)S(1)} collective-permute-done((f32[128,128]{1,0:T(8,128)S(1)}, f32[128,128]{1,0:T(8,128)S(1)}, u32[]{:S(2)}, u32[]{:S(2)}) %collective-permute-start.3) | collective-permute-done | bytes 65568 | tf_op jit(solution)/shard_map/ppermute | solution.py:27
  55.9 9.1 %all_to_all.33 = f32[4,128,128]{2,1,0:T(8,128)S(1)} all-to-all(f32[4,128,128]{2,1,0:T(8,128)S(1)} %broadcast_in_dim.4), channel_id=1, replica_groups=mesh['sub'=64,'grp'=4] {'grp'}, dimensions={0} | all-to-all | bytes 524288 | tf_op jit(solution)/shard_map/all_to_all | solution.py:17
  65.5 3.4 %collective-permute-done.5 = f32[512,128]{1,0:T(8,128)S(1)} collective-permute-done((f32[512,128]{1,0:T(8,128)S(1)}, f32[512,128]{1,0:T(8,128)S(1)}, u32[]{:S(2)}, u32[]{:S(2)}) %collective-permute-start.5) | collective-permute-done | bytes 262176 | tf_op jit(solution)/shard_map/ppermute | solution.py:27
  68.9 5.2 %collective-permute-done.4 = f32[512,128]{1,0:T(8,128)S(1)} collective-permute-done((f32[512,128]{1,0:T(8,128)S(1)}, f32[512,128]{1,0:T(8,128)S(1)}, u32[]{:S(2)}, u32[]{:S(2)}) %collective-permute-start.4) | collective-permute-done | bytes 262176 | tf_op jit(solution)/shard_map/ppermute | solution.py:27
  76.1 9.1 %all_to_all.34 = f32[4,128,128]{2,1,0:T(8,128)S(1)} all-to-all(f32[4,128,128]{2,1,0:T(8,128)S(1)} %fusion.32), channel_id=1, replica_groups=mesh['sub'=64,'grp'=4] {'grp'}, dimensions={0} | all-to-all | bytes 524288 | tf_op jit(solution)/shard_map/all_to_all | solution.py:77
  85.8 1.4 %collective-permute-done.6 = f32[128,128]{1,0:T(8,128)S(1)} collective-permute-done((f32[128,128]{1,0:T(8,128)S(1)}, f32[128,128]{1,0:T(8,128)S(1)}, u32[]{:S(2)}, u32[]{:S(2)}) %collective-permute-start.6) | collective-permute-done | bytes 65568 | tf_op jit(solution)/shard_map/ppermute | solution.py:27
  87.2 5.2 %collective-permute-done.7 = f32[128,128]{1,0:T(8,128)S(1)} collective-permute-done((f32[128,128]{1,0:T(8,128)S(1)}, f32[128,128]{1,0:T(8,128)S(1)}, u32[]{:S(2)}, u32[]{:S(2)}) %collective-permute-start.7) | collective-permute-done | bytes 65568 | tf_op jit(solution)/shard_map/ppermute | solution.py:27
  92.5 9.1 %all_to_all.35 = f32[4,128,128]{2,1,0:T(8,128)S(1)} all-to-all(f32[4,128,128]{2,1,0:T(8,128)S(1)} %broadcast_in_dim.5), channel_id=1, replica_groups=mesh['sub'=64,'grp'=4] {'grp'}, dimensions={0} | all-to-all | bytes 524288 | tf_op jit(solution)/shard_map/all_to_all | solution.py:17
  102.1 3.4 %collective-permute-done.9 = f32[512,128]{1,0:T(8,128)S(1)} collective-permute-done((f32[512,128]{1,0:T(8,128)S(1)}, f32[512,128]{1,0:T(8,128)S(1)}, u32[]{:S(2)}, u32[]{:S(2)}) %collective-permute-start.9) | collective-permute-done | bytes 262176 | tf_op jit(solution)/shard_map/ppermute | solution.py:27
  105.4 5.2 %collective-permute-done.8 = f32[512,128]{1,0:T(8,128)S(1)} collective-permute-done((f32[512,128]{1,0:T(8,128)S(1)}, f32[512,128]{1,0:T(8,128)S(1)}, u32[]{:S(2)}, u32[]{:S(2)}) %collective-permute-start.8) | collective-permute-done | bytes 262176 | tf_op jit(solution)/shard_map/ppermute | solution.py:27
  111.7 1.0 fusion.33
  112.7 9.1 %all_to_all.36 = f32[4,128,128]{2,1,0:T(8,128)S(1)} all-to-all(f32[4,128,128]{2,1,0:T(8,128)S(1)} %fusion.33), channel_id=1, replica_groups=mesh['sub'=64,'grp'=4] {'grp'}, dimensions={0} | all-to-all | bytes 524288 | tf_op jit(solution)/shard_map/all_to_all | solution.py:77
  122.4 1.4 %collective-permute-done.10 = f32[128,128]{1,0:T(8,128)S(1)} collective-permute-done((f32[128,128]{1,0:T(8,128)S(1)}, f32[128,128]{1,0:T(8,128)S(1)}, u32[]{:S(2)}, u32[]{:S(2)}) %collective-permute-start.10) | collective-permute-done | bytes 65568 | tf_op jit(solution)/shard_map/ppermute | solution.py:27
  123.8 5.2 %collective-permute-done.11 = f32[128,128]{1,0:T(8,128)S(1)} collective-permute-done((f32[128,128]{1,0:T(8,128)S(1)}, f32[128,128]{1,0:T(8,128)S(1)}, u32[]{:S(2)}, u32[]{:S(2)}) %collective-permute-start.11) | collective-permute-done | bytes 65568 | tf_op jit(solution)/shard_map/ppermute | solution.py:27
  (40 shorter events, 8.7 us)
Async XLA Ops:
  0.0 15.8 %copy-start = (bf16[1,2048,512]{2,1,0:T(8,128)(2,1)S(1)}, bf16[1,2048,512]{2,1,0:T(8,128)(2,1)}, u32[]{:S(2)}) copy-start(bf16[1,2048,512]{2,1,0:T(8,128)(2,1)} %param.7) | copy-start | bytes 6291460
  1.1 30.8 %collective-permute-start.1 = (f32[512,128]{1,0:T(8,128)S(1)}, f32[512,128]{1,0:T(8,128)}, u32[]{:S(2)}, u32[]{:S(2)}) collective-permute-start(f32[512,128]{1,0:T(8,128)S(1)} %convert_element_type.44), channel_id=1, source_target_pairs={{4,0},{8,4},{12,8},{16,12},{20,16},{24,20},{28,24},{32,28},{36,32}... | collective-permute-start | bytes 786440 | tf_op jit(solution)/shard_map/ppermute | solution.py:27
  8.9 22.9 %collective-permute-start = (f32[512,128]{1,0:T(8,128)S(1)}, f32[512,128]{1,0:T(8,128)}, u32[]{:S(2)}, u32[]{:S(2)}) collective-permute-start(f32[512,128]{1,0:T(8,128)S(1)} %convert_element_type.44), channel_id=1, source_target_pairs={{252,0},{0,4},{4,8},{8,12},{12,16},{16,20},{20,24},{24,28},{28,32}... | collective-permute-start | bytes 786440 | tf_op jit(solution)/shard_map/ppermute | solution.py:27
  10.2 25.3 %all-to-all-start.1 = ((f32[4,1,1]{2,1,0:T(1,128)}), f32[4,1,1]{2,1,0:T(1,128)S(1)}, u32[]{:S(2)}, u32[]{:S(2)}) async-start(f32[4,1,1]{2,1,0:T(1,128)} %copy.22), calls=%async_computation.1 | async-start | bytes 4096 | tf_op jit(solution)/shard_map/all_to_all | solution.py:78
  15.8 16.0 %copy-start.1 = (s32[1,4]{1,0:T(1,128)S(1)}, s32[1,4]{1,0:T(1,128)}, u32[]{:S(2)}) copy-start(s32[1,4]{1,0:T(1,128)} %param.10) | copy-start | bytes 52
  35.6 10.0 %all-to-all-start = ((f32[4,128,128]{2,1,0:T(8,128)}), f32[4,128,128]{2,1,0:T(8,128)S(1)}, u32[]{:S(2)}, u32[]{:S(2)}) async-start(f32[4,128,128]{2,1,0:T(8,128)} %fusion.31), calls=%async_computation | async-start | bytes 524288 | tf_op jit(solution)/shard_map/all_to_all | solution.py:77
  45.7 5.0 %collective-permute-start.2 = (f32[128,128]{1,0:T(8,128)S(1)}, f32[128,128]{1,0:T(8,128)S(1)}, u32[]{:S(2)}, u32[]{:S(2)}) collective-permute-start(f32[128,128]{1,0:T(8,128)S(1)} %get-tuple-element.11), channel_id=1, source_target_pairs={{4,0},{8,4},{12,8},{16,12},{20,16},{24,20},{28,24},{32,28},{36,32}... | collective-permute-start | bytes 196616 | tf_op jit(solution)/shard_map/ppermute | solution.py:27
  48.8 7.0 %collective-permute-start.3 = (f32[128,128]{1,0:T(8,128)S(1)}, f32[128,128]{1,0:T(8,128)S(1)}, u32[]{:S(2)}, u32[]{:S(2)}) collective-permute-start(f32[128,128]{1,0:T(8,128)S(1)} %get-tuple-element.12), channel_id=1, source_target_pairs={{252,0},{0,4},{4,8},{8,12},{12,16},{16,20},{20,24},{24,28},{28,32}... | collective-permute-start | bytes 196616 | tf_op jit(solution)/shard_map/ppermute | solution.py:27
  65.0 3.9 %collective-permute-start.5 = (f32[512,128]{1,0:T(8,128)S(1)}, f32[512,128]{1,0:T(8,128)S(1)}, u32[]{:S(2)}, u32[]{:S(2)}) collective-permute-start(f32[512,128]{1,0:T(8,128)S(1)} %bitcast.73), channel_id=1, source_target_pairs={{4,0},{8,4},{12,8},{16,12},{20,16},{24,20},{28,24},{32,28},{36,32}... | collective-permute-start | bytes 786440 | tf_op jit(solution)/shard_map/ppermute | solution.py:27
  65.0 9.1 %collective-permute-start.4 = (f32[512,128]{1,0:T(8,128)S(1)}, f32[512,128]{1,0:T(8,128)S(1)}, u32[]{:S(2)}, u32[]{:S(2)}) collective-permute-start(f32[512,128]{1,0:T(8,128)S(1)} %bitcast.74), channel_id=1, source_target_pairs={{252,0},{0,4},{4,8},{8,12},{12,16},{16,20},{20,24},{24,28},{28,32}... | collective-permute-start | bytes 786440 | tf_op jit(solution)/shard_map/ppermute | solution.py:27
  85.3 2.0 %collective-permute-start.6 = (f32[128,128]{1,0:T(8,128)S(1)}, f32[128,128]{1,0:T(8,128)S(1)}, u32[]{:S(2)}, u32[]{:S(2)}) collective-permute-start(f32[128,128]{1,0:T(8,128)S(1)} %get-tuple-element.8), channel_id=1, source_target_pairs={{4,0},{8,4},{12,8},{16,12},{20,16},{24,20},{28,24},{32,28},{36,32}... | collective-permute-start | bytes 196616 | tf_op jit(solution)/shard_map/ppermute | solution.py:27
  85.4 7.1 %collective-permute-start.7 = (f32[128,128]{1,0:T(8,128)S(1)}, f32[128,128]{1,0:T(8,128)S(1)}, u32[]{:S(2)}, u32[]{:S(2)}) collective-permute-start(f32[128,128]{1,0:T(8,128)S(1)} %get-tuple-element.9), channel_id=1, source_target_pairs={{252,0},{0,4},{4,8},{8,12},{12,16},{16,20},{20,24},{24,28},{28,32}... | collective-permute-start | bytes 196616 | tf_op jit(solution)/shard_map/ppermute | solution.py:27
  101.5 3.9 %collective-permute-start.9 = (f32[512,128]{1,0:T(8,128)S(1)}, f32[512,128]{1,0:T(8,128)S(1)}, u32[]{:S(2)}, u32[]{:S(2)}) collective-permute-start(f32[512,128]{1,0:T(8,128)S(1)} %bitcast.76), channel_id=1, source_target_pairs={{4,0},{8,4},{12,8},{16,12},{20,16},{24,20},{28,24},{32,28},{36,32}... | collective-permute-start | bytes 786440 | tf_op jit(solution)/shard_map/ppermute | solution.py:27
  101.6 9.1 %collective-permute-start.8 = (f32[512,128]{1,0:T(8,128)S(1)}, f32[512,128]{1,0:T(8,128)S(1)}, u32[]{:S(2)}, u32[]{:S(2)}) collective-permute-start(f32[512,128]{1,0:T(8,128)S(1)} %bitcast.77), channel_id=1, source_target_pairs={{252,0},{0,4},{4,8},{8,12},{12,16},{16,20},{20,24},{24,28},{28,32}... | collective-permute-start | bytes 786440 | tf_op jit(solution)/shard_map/ppermute | solution.py:27
  121.8 2.0 %collective-permute-start.10 = (f32[128,128]{1,0:T(8,128)S(1)}, f32[128,128]{1,0:T(8,128)S(1)}, u32[]{:S(2)}, u32[]{:S(2)}) collective-permute-start(f32[128,128]{1,0:T(8,128)S(1)} %get-tuple-element.5), channel_id=1, source_target_pairs={{4,0},{8,4},{12,8},{16,12},{20,16},{24,20},{28,24},{32,28},{36,32}... | collective-permute-start | bytes 196616 | tf_op jit(solution)/shard_map/ppermute | solution.py:27
  121.9 7.1 %collective-permute-start.11 = (f32[128,128]{1,0:T(8,128)S(1)}, f32[128,128]{1,0:T(8,128)S(1)}, u32[]{:S(2)}, u32[]{:S(2)}) collective-permute-start(f32[128,128]{1,0:T(8,128)S(1)} %get-tuple-element.6), channel_id=1, source_target_pairs={{252,0},{0,4},{4,8},{8,12},{12,16},{16,20},{20,24},{24,28},{28,32}... | collective-permute-start | bytes 196616 | tf_op jit(solution)/shard_map/ppermute | solution.py:27
where the time goes:
time: 130 us
  waiting for transfers between devices  42.5 us (33%)
  blocking collectives  36.3 us (28%)
  starting transfers between devices  22.8 us (18%)
  matrix products  22.3 us (17%)
  other arithmetic  4.09 us (3%)
    ppermute x12, waiting for transfers between devices, passed_along(): return lax.ppermute(block, axis, route)  37.4 us
    all_to_all x2, blocking collectives, sent_to_all(): return lax.all_to_all(copies, axis, split_axis=0, concat_axis=0, tiled=True)  18.1 us
    all_to_all x2, blocking collectives, local(): lax.all_to_all(product, 'grp', split_axis=0, concat_axis=0, tiled=True)  18.1 us
    dot_general x1, matrix products, local(): lax.dot_general(coupled, coupled, (((0,), (0,)), ((), ())), preferred_ele...  16 us
    ppermute x12, starting transfers between devices, passed_along(): return lax.ppermute(block, axis, route)  13.1 us
    all_to_all x1, waiting for transfers between devices, local(): lax.all_to_all(product, 'grp', split_axis=0, concat_axis=0, tiled=True)  5.1 us
    all_to_all x1, starting transfers between devices, local(): lax.all_to_all(dest.astype(jnp.float32), 'grp', split_axis=0, concat_axis...  4.82 us
    all_to_all x1, starting transfers between devices, local(): lax.all_to_all(product, 'grp', split_axis=0, concat_axis=0, tiled=True)  4.8 us
  transfers between devices with their start and end apart: 14, of which 11 were waited for; matrix products, arithmetic and copies ran while one was open for 16% of the time, Pallas kernels for 0%

commit v1 on v0

v1 whole, which is shorter than its diff:
```python
import functools

import jax
import jax.numpy as jnp
from jax import lax
from jax.experimental import pallas as pl
from jax.experimental.pallas import tpu as pltpu
from jax.sharding import PartitionSpec as P

POWER = 3
CHUNKS = 2
MESH = pl.DeviceIdType.MESH


def halves(x):
    hi = x.astype(jnp.bfloat16)
    lo = (x - hi.astype(jnp.float32)).astype(jnp.bfloat16)
    return hi, lo


def body(
    cycles,
    groups,
    factor_hbm,
    coupling_hbm,
    block_hbm,
    panel_hbm,
    ids_hbm,
    count_hbm,
    out_ref,
    factor,
    coupling,
    block,
    panel,
    ids,
    count,
    coupled,
    m_hi,
    m_lo,
    halo,
    idx_mine,
    idx_far,
    p_mine,
    p_far,
    t_mine,
    near_low,
    near_high,
    far_low,
    far_high,
    v_mine,
    x_all,
    v_last,
    in_sems,
    halo_send,
    halo_recv,
    idx_send,
    idx_recv,
    p_send,
    p_recv,
    t_send,
    t_recv,
    v_send,
    v_recv,
):
    home = lax.axis_index("sub")
    mine = lax.axis_index("grp")
    size = factor.shape[0]
    width = block.shape[0]
    blk = width // groups
    samples = panel.shape[1]
    part = samples // CHUNKS
    rows = min(256, size)
    tiles = size // rows

    def ring(step):
        return lax.rem(home + step + cycles, cycles)

    def member(step):
        return lax.rem(mine + step, groups)

    loads = [
        pltpu.make_async_copy(ids_hbm, ids, in_sems.at[0]),
        pltpu.make_async_copy(count_hbm, count, in_sems.at[1]),
        pltpu.make_async_copy(panel_hbm, panel, in_sems.at[2]),
    ]
    for load in loads:
        load.start()
    factor_loads, coupling_loads = [], []
    for i in range(tiles):
        span = pl.ds(i * rows, rows)
        edge = pl.ds(0, (i + 1) * rows)
        coupling_loads.append(
            pltpu.make_async_copy(
                coupling_hbm.at[span, :], coupling.at[span, :], in_sems.at[4 + 2 * i]
            )
        )
        factor_loads.append(
            pltpu.make_async_copy(
                factor_hbm.at[span, edge], factor.at[span, edge], in_sems.at[5 + 2 * i]
            )
        )
        coupling_loads[i].start()
        factor_loads[i].start()
    block_load = pltpu.make_async_copy(block_hbm, block, in_sems.at[3])
    block_load.start()

    barrier = pltpu.get_barrier_semaphore()
    partners = [(ring(s), mine) for s in (-2, -1, 1, 2)]
    partners += [(home, member(r)) for r in range(1, groups)]
    for partner in partners:
        pl.semaphore_signal(barrier, inc=1, device_id=partner, device_id_type=MESH)

    for load in loads:
        load.wait()
    for b in range(groups):
        rows_b = panel[b * blk : (b + 1) * blk, :].astype(jnp.float32).T
        for c in range(CHUNKS):
            halo[c, 1, b] = rows_b[c * part : (c + 1) * part, :]
    for a in range(groups):
        owner = ids[0, a] // groups
        away = lax.rem(owner - home + cycles + 1, cycles) - 1
        idx_mine[a] = jnp.full((8, 128), away, jnp.int32)

    def couple(i):
        coupling_loads[i].wait()
        factor_loads[i].wait()
        span = slice(i * rows, (i + 1) * rows)
        coupled[span, :] = jnp.dot(
            factor[span, : (i + 1) * rows],
            coupling[: (i + 1) * rows, :],
            preferred_element_type=jnp.float32,
        ).astype(jnp.bfloat16)

    early = min(3, tiles)
    for i in range(early):
        couple(i)

    pl.semaphore_wait(barrier, len(partners))
    sent = []

    def send(src, dst, send_sem, recv_sem, device):
        copy = pltpu.make_async_remote_copy(
            src_ref=src,
            dst_ref=dst,
            send_sem=send_sem,
            recv_sem=recv_sem,
            device_id=device,
            device_id_type=MESH,
        )
        copy.start()
        sent.append(copy)
        return copy

    idx_copies = []
    for r in range(1, groups):
        idx_copies.append(
            send(
                idx_mine.at[member(r)],
                idx_far.at[r - 1],
                idx_send.at[r - 1],
                idx_recv.at[r - 1],
                (home, member(r)),
            )
        )
    halo_copies = []
    for c in range(CHUNKS):
        up = send(
            halo.at[c, 1], halo.at[c, 0], halo_send.at[c, 0], halo_recv.at[c, 0], (ring(1), mine)
        )
        down = send(
            halo.at[c, 1], halo.at[c, 2], halo_send.at[c, 1], halo_recv.at[c, 1], (ring(-1), mine)
        )
        halo_copies.append((up, down))

    for i in range(early, tiles):
        couple(i)

    block_load.wait()
    live = count[0]
    for a in range(groups):
        span = slice(a * blk, (a + 1) * blk)
        gram = lax.dot_general(
            coupled[:, span],
            coupled[...],
            (((0,), (0,)), ((), ())),
            preferred_element_type=jnp.float32,
        )
        schur = block[span, :] - gram
        column = lax.broadcasted_iota(jnp.int32, (blk, width), 1) // blk
        limit = jnp.where(a < live, live, 0)
        schur = jnp.where(column < limit, schur, 0.0)
        hi, lo = halves(schur)
        m_hi[span, :] = hi
        m_lo[span, :] = lo

    def pick(index, low, mid, high):
        index = index[None]
        return jnp.where(index == 0, mid, jnp.where(index < 0, low, high))

    def tiled(x):
        return x.reshape(x.shape[0] // 8, 8, x.shape[1])

    def flat(x):
        return x.reshape(x.shape[0] * 8, x.shape[2])

    def apply(x):
        hi, lo = halves(x)
        both = jnp.concatenate([hi, lo], axis=0)
        top = jnp.dot(both, m_hi[...], preferred_element_type=jnp.float32)
        low = jnp.dot(hi, m_lo[...], preferred_element_type=jnp.float32)
        return top[:part] + (top[part:] + low)

    def spread(t, c, x):
        product = apply(x)
        copies = []
        for a in range(groups):
            p_mine[t, c, a] = product[:, a * blk : (a + 1) * blk]
        for r in (2, 1, 3):
            copies.append(
                send(
                    p_mine.at[t, c, member(r)],
                    p_far.at[t, c, r - 1],
                    p_send.at[t, c, r - 1],
                    p_recv.at[t, c, r - 1],
                    (home, member(r)),
                )
            )
        return copies

    def first_x(c):
        up, down = halo_copies[c]
        up.wait_recv()
        down.wait_recv()
        pieces = []
        for b in range(groups):
            x = pick(
                idx_mine[b], tiled(halo[c, 0, b]), tiled(halo[c, 1, b]), tiled(halo[c, 2, b])
            )
            pieces.append(flat(x))
        return jnp.concatenate(pieces, axis=1)

    def next_x(t, c):
        return jnp.concatenate([x_all[t, c, b] for b in range(groups)], axis=1)

    def totals(t, c, copies):
        terms = [tiled(p_mine[t, c, mine])]
        where = [idx_mine[mine]]
        for copy in copies:
            copy.wait_recv()
        for r in range(1, groups):
            terms.append(tiled(p_far[t, c, r - 1]))
            where.append(idx_far[r - 1])
        out = []
        for e in (-1, 0, 1):
            total = None
            for term, index in zip(terms, where):
                kept = jnp.where(index[None] == e, term, 0.0)
                total = kept if total is None else total + kept
            out.append(flat(total))
        return out

    def pass_on(t, c, copies):
        low, mid, high = totals(t, c, copies)
        t_mine[t, c, 0] = low
        t_mine[t, c, 1] = mid
        t_mine[t, c, 2] = high
        if t == POWER - 1:
            return [
                send(
                    t_mine.at[t, c, 2],
                    near_low.at[t, c, 0],
                    t_send.at[t, c, 0],
                    t_recv.at[t, c, 0],
                    (ring(1), mine),
                ),
                send(
                    t_mine.at[t, c, 0],
                    near_high.at[t, c, 0],
                    t_send.at[t, c, 1],
                    t_recv.at[t, c, 1],
                    (ring(-1), mine),
                ),
            ]
        return [
            send(
                t_mine.at[t, c, pl.ds(1, 2)],
                near_low.at[t, c],
                t_send.at[t, c, 0],
                t_recv.at[t, c, 0],
                (ring(1), mine),
            ),
            send(
                t_mine.at[t, c, pl.ds(0, 2)],
                near_high.at[t, c],
                t_send.at[t, c, 1],
                t_recv.at[t, c, 1],
                (ring(-1), mine),
            ),
            send(
                t_mine.at[t, c, 2],
                far_low.at[t, c],
                t_send.at[t, c, 2],
                t_recv.at[t, c, 2],
                (ring(2), mine),
            ),
            send(
                t_mine.at[t, c, 0],
                far_high.at[t, c],
                t_send.at[t, c, 3],
                t_recv.at[t, c, 3],
                (ring(-2), mine),
            ),
        ]

    def choose(t, c, copies):
        for copy in copies:
            copy.wait_recv()
        low = tiled(0.5 * (t_mine[t, c, 0] + near_low[t, c, 0] + far_low[t, c]))
        mid = tiled(0.5 * (t_mine[t, c, 1] + near_low[t, c, 1] + near_high[t, c, 0]))
        high = tiled(0.5 * (t_mine[t, c, 2] + near_high[t, c, 1] + far_high[t, c]))
        out = []
        for r in (2, 1, 3):
            v_mine[t, c, r - 1] = flat(pick(idx_far[groups - r - 1], low, mid, high))
            out.append(
                send(
                    v_mine.at[t, c, r - 1],
                    x_all.at[t + 1, c, mine],
                    v_send.at[t, c, r - 1],
                    v_recv.at[t, c, r - 1],
                    (home, member(r)),
                )
            )
        x_all[t + 1, c, mine] = flat(pick(idx_mine[mine], low, mid, high))
        return out

    chunks = range(CHUNKS)
    moving = [spread(0, c, first_x(c)) for c in chunks]
    for copy in idx_copies:
        copy.wait_recv()
    for t in range(POWER):
        moving = [pass_on(t, c, moving[c]) for c in chunks]
        if t == POWER - 1:
            break
        moving = [choose(t, c, moving[c]) for c in chunks]
        following = []
        for c in chunks:
            for copy in moving[c]:
                copy.wait_recv()
            following.append(spread(t + 1, c, next_x(t + 1, c)))
        moving = following
    last = POWER - 1
    for c in chunks:
        for copy in moving[c]:
            copy.wait_recv()
        v_last[c * part : (c + 1) * part, :] = (
            t_mine[last, c, 1] + near_low[last, c, 0] + near_high[last, c, 0]
        )
    out_ref[...] = 0.5 * v_last[...].T
    for copy in sent:
        copy.wait_send()


def local(
    interior_factor, interface_coupling, interface_block, sample_panel, index_map, block_count
):
    cycles = lax.axis_size("sub")
    groups = lax.axis_size("grp")
    size = interior_factor.shape[1]
    width = interface_block.shape[1]
    blk = width // groups
    samples = sample_panel.shape[1]
    part = samples // CHUNKS
    f32, bf16 = jnp.float32, jnp.bfloat16
    dma = pltpu.SemaphoreType.DMA
    tiles = size // min(256, size)

    def vmem(*shape, dtype=f32):
        return pltpu.VMEM(shape, dtype)

    scratch = [
        vmem(size, size, dtype=bf16),
        vmem(size, width, dtype=bf16),
        vmem(width, width),
        vmem(width, samples, dtype=bf16),
        pltpu.SMEM((1, groups), jnp.int32),
        pltpu.SMEM((1,), jnp.int32),
        vmem(size, width, dtype=bf16),
        vmem(width, width, dtype=bf16),
        vmem(width, width, dtype=bf16),
        vmem(CHUNKS, 3, groups, part, blk),
        vmem(groups, 8, 128, dtype=jnp.int32),
        vmem(groups - 1, 8, 128, dtype=jnp.int32),
        vmem(POWER, CHUNKS, groups, part, blk),
        vmem(POWER, CHUNKS, groups - 1, part, blk),
        vmem(POWER, CHUNKS, 3, part, blk),
        vmem(POWER, CHUNKS, 2, part, blk),
        vmem(POWER, CHUNKS, 2, part, blk),
        vmem(POWER, CHUNKS, part, blk),
        vmem(POWER, CHUNKS, part, blk),
        vmem(POWER, CHUNKS, groups - 1, part, blk),
        vmem(POWER, CHUNKS, groups, part, blk),
        vmem(samples, blk),
        dma((4 + 2 * tiles,)),
        dma((CHUNKS, 2)),
        dma((CHUNKS, 2)),
        dma((groups - 1,)),
        dma((groups - 1,)),
        dma((POWER, CHUNKS, groups - 1)),
        dma((POWER, CHUNKS, groups - 1)),
        dma((POWER, CHUNKS, 4)),
        dma((POWER, CHUNKS, 4)),
        dma((POWER, CHUNKS, groups - 1)),
        dma((POWER, CHUNKS, groups - 1)),
    ]
    return pl.pallas_call(
        functools.partial(body, cycles, groups),
        out_shape=jax.ShapeDtypeStruct((blk, samples), f32),
        in_specs=[pl.BlockSpec(memory_space=pl.ANY)] * 6,
        out_specs=pl.BlockSpec(memory_space=pltpu.VMEM),
        scratch_shapes=scratch,
        compiler_params=pltpu.CompilerParams(collective_id=0, has_side_effects=True),
        name="power_steps",
    )(
        interior_factor[0],
        interface_coupling[0],
        interface_block[0],
        sample_panel,
        index_map,
        block_count,
    )


def solution(mesh):
    return jax.shard_map(
        local,
        mesh=mesh,
        in_specs=(
            P(("sub", "grp"), None, None),
            P(("sub", "grp"), None, None),
            P(("sub", "grp"), None, None),
            P("sub", None),
            P(("sub", "grp"), None),
            P(("sub", "grp")),
        ),
        out_specs=P(("sub", "grp"), None),
        check_vma=False,
    )
```

time: 130 us -> 53.1 us (0.41)
  Pallas kernels: 0 us -> 50.2 us
  waiting for transfers between devices: 42.5 us -> 0 us
  blocking collectives: 36.3 us -> 0 us
  starting transfers between devices: 22.8 us -> 0 us
  matrix products: 22.3 us -> 0 us
  other arithmetic: 4.09 us -> 0 us
    pallas_call x0 -> x1, Pallas kernels: none -> 50.2 us  [local(): pl.pallas_call(functools.partial(body, cycles, groups), out_shape=jax.Sha...]
    ppermute x12 -> x0, waiting for transfers between devices: 37.4 us -> none  [passed_along(): return lax.ppermute(block, axis, route)]
    all_to_all x4 -> x0, blocking collectives: 36.3 us -> none  [the longest x2 18.1 us: sent_to_all(): return lax.all_to_all(copies, axis, split_axis=0, concat_axis=0, tiled=True)]
    dot_general x7 -> x0, matrix products: 22.3 us -> none  [the longest x1 16 us: local(): lax.dot_general(coupled, coupled, (((0,), (0,)), ((), ())), preferred_ele...]
    ppermute x12 -> x0, starting transfers between devices: 13.1 us -> none  [passed_along(): return lax.ppermute(block, axis, route)]
    all_to_all x2 -> x0, starting transfers between devices: 9.62 us -> none  [the longest x1 4.82 us: local(): lax.all_to_all(dest.astype(jnp.float32), 'grp', split_axis=0, concat_axis...]
    all_to_all x2 -> x0, waiting for transfers between devices: 5.11 us -> none  [the longest x1 5.1 us: local(): lax.all_to_all(product, 'grp', split_axis=0, concat_axis=0, tiled=True)]
    convert_element_type x3 -> x0, other arithmetic: 1.75 us -> none  [the longest x1 1.07 us: local(): current = sample_panel.astype(jnp.float32)]
  transfers between devices with their start and end apart: 14 -> 0, of which waited for: 11 -> 0; matrix products, arithmetic and copies ran while one was open for 16% -> 0% of each run, Pallas kernels for 0% -> 0%
where the time goes in v1:
time: 53.1 us; the launch traced here: 52.4 us
  Pallas kernels  50.2 us (95%)
  local copies, waits for them, and re-layouts  1.47 us (3%)
  between operations  0.66 us (1%)
    pallas_call x1, Pallas kernels, local(): pl.pallas_call(functools.partial(body, cycles, groups), out_shape=jax.Sha...  50.2 us
    unnamed x1, local copies, waits for them, and re-layouts  1.47 us

profile of v1, /device:TPU:2, one launch (start us, length us, event | category | flops | bytes accessed | tf_op | source)
XLA Modules:
  0.0 52.4 jit_solution(11715626841399286372)
XLA Ops:
  0.7 50.2 %power_steps.1 = f32[128,128]{1,0:T(8,128)} custom-call(bf16[2048,2048]{1,0:T(8,128)(2,1)} %bitcast.3, bf16[2048,512]{1,0:T(8,128)(2,1)} %bitcast.4, f32[512,512]{1,0:T(8,128)} %bitcast.5, bf16[512,128]{1,0:T(8,128)(2,1)} %panel_hbm.1, s32[1,4]{1,0:T(1,128)} %ids_hbm.1, s32[1]{0:T(128)S(6)} %copy.8.count_hbm), custom_call_target="tpu_custom_call" | custom-call | tf_op jit(solution)/shard_map/power_steps/pallas_call | solution.py:415
  50.9 1.5 %copy.9 = f32[128,128]{1,0:T(8,128)} copy(f32[128,128]{1,0:T(8,128)} %power_steps.1) | data formatting | bytes 131072
